TPU v7x, 32 devices: a whole 2x2x4 slice. The times are simulated.
32 devices in a mesh: fsdp: 16 (over z, y, x), model: 2 (over core).
Axes of the slice: x: 2, y: 2, z: 4, core: 2. Of those that a mesh axis runs over, the one named last changes fastest.
Arguments:
- train_query: float32 [2560, 4096], P('fsdp', 'model'), may hold values from -0.15625 to 0.15625
- drift_query: float32 [2560, 4096], P('fsdp', 'model'), may hold values from -6 to 6
- spread_query: float32 [2560, 4096], P('fsdp', 'model'), may hold values from 0.1 to 10
- train_key: float32 [2560, 1024], P('fsdp', 'model'), may hold values from -0.15625 to 0.15625
- drift_key: float32 [2560, 1024], P('fsdp', 'model'), may hold values from -6 to 6
- spread_key: float32 [2560, 1024], P('fsdp', 'model'), may hold values from 0.1 to 10
- train_value: float32 [2560, 1024], P('fsdp', 'model'), may hold values from -0.15625 to 0.15625
- drift_value: float32 [2560, 1024], P('fsdp', 'model'), may hold values from -6 to 6
- spread_value: float32 [2560, 1024], P('fsdp', 'model'), may hold values from 0.1 to 10
- norm_train: float32 [2560], P(('fsdp', 'model')), may hold values from 0.25 to 1.75
- norm_step: float32 [2560], P(('fsdp', 'model')), may hold values from -0.3 to 0.3
Outputs:
- serve_query: bfloat16 [2560, 4096], P(None, 'model')
- serve_key: bfloat16 [2560, 1024], P(None, 'model')
- serve_value: bfloat16 [2560, 1024], P(None, 'model')
- factor_query: float32 [4096], P('model')
- factor_key: float32 [1024], P('model')
- factor_value: float32 [1024], P('model')
- serve_norm: bfloat16 [2560], replicated
- fresh_query: float32 [2560, 4096], P('fsdp', 'model')
- fresh_key: float32 [2560, 1024], P('fsdp', 'model')
- fresh_value: float32 [2560, 1024], P('fsdp', 'model')
All inputs are finite; a program needn't handle non-finite values. Where the computation divides by a largest or mean magnitude, that divisor is 1e-20 or more.
Results may differ from a plain program's by a relative error of at most 0.001.
Values may be sent and summed in bfloat16 or wider, within the bound.
A program may use at most 64 MiB of HBM per device.

v0:
```python
import functools

import jax
import jax.numpy as jnp
from jax import lax
from jax.experimental import pallas as pl
from jax.experimental.pallas import tpu as pltpu
from jax.sharding import PartitionSpec as P

learn_rate = 0.02
decay_rate = 0.05
tiny_value = 1e-08
MESH = pl.DeviceIdType.MESH
ROWS = 16
CHUNK = 32
VMEM_BYTES = 67043328
LANES = 128

AZ, BZ, AX, AXF, AY, AYF, BXF, BYF, COUNT = 0, 4, 20, 24, 28, 32, 36, 37, 38


def stepped(train, drift, spread):
    return train - learn_rate * (drift / (jnp.sqrt(spread) + tiny_value) + decay_rate * train)


def gather_kernel(
    part_a,
    tq, dq, sq, tk, dk, sk, tv, dv, sv, norm_train, norm_step,
    held, fresh_q, fresh_k, fresh_v, factor, norms,
    in_q, in_k, in_v, norm_in, top, early_q, early_k, early_v,
    mx, in_sem, norm_sem, mx_send, mx_recv, nm_send, nm_recv, early_send, early_recv, send, recv,
):
    f = lax.axis_index("fsdp")
    m = lax.axis_index("model")
    z = f // 4
    r = f % 4
    y = r // 2
    x = r % 2
    rx, ry, rd = y * 2 + (1 - x), (1 - y) * 2 + x, (1 - y) * 2 + (1 - x)
    rows = fresh_q.shape[0]
    widths = (fresh_q.shape[1], fresh_k.shape[1], fresh_v.shape[1])
    starts = (0, widths[0], widths[0] + widths[1])
    fresh = (fresh_q, fresh_k, fresh_v)
    early = (early_q, early_k, early_v)
    inputs = ((tq, dq, sq), (tk, dk, sk), (tv, dv, sv))
    local = (in_q, in_k, in_v)
    half_a = part_a // 2
    half_b = (rows - part_a) // 2

    def device(zz, rr):
        return {"fsdp": zz * 4 + rr, "model": m}

    plane = [device(z, rx), device(z, ry), device(z, rd)]
    line = [device((z + k) % 4, r) for k in range(1, 4)]
    partner = {"fsdp": f, "model": 1 - m}

    barrier = pltpu.get_barrier_semaphore()
    for peer in plane + line + [partner]:
        pl.semaphore_signal(barrier, inc=1, device_id=peer, device_id_type=MESH)

    def loads(i):
        at = pl.ds(pl.multiple_of(i * CHUNK, CHUNK), CHUNK)
        return [
            pltpu.make_async_copy(src.at[at], local[a].at[k, at], in_sem.at[i, a * 3 + k])
            for a in range(3)
            for k, src in enumerate(inputs[a])
        ]

    for i in range(rows // CHUNK):
        for copy in loads(i):
            copy.start()
    norm_loads = [
        pltpu.make_async_copy(src, norm_in.at[k], norm_sem.at[k])
        for k, src in enumerate((norm_train, norm_step))
    ]
    for copy in norm_loads:
        copy.start()

    top[...] = jnp.zeros_like(top)

    def chunk(i, carry):
        copies = loads(i)
        for a, (ref, start, width) in enumerate(zip(fresh, starts, widths)):
            for copy in copies[a * 3 : a * 3 + 3]:
                copy.wait()
            step = min(512, width)
            for c in range(0, width, step):
                cols = slice(c, c + step)
                best = top[:, start + c : start + c + step]
                for g in range(CHUNK // 8):
                    at = pl.ds(pl.multiple_of(i * CHUNK + g * 8, 8), 8)
                    new = stepped(local[a][0, at, cols], local[a][1, at, cols], local[a][2, at, cols])
                    ref[at, cols] = new
                    best = jnp.maximum(best, jnp.abs(new))
                top[:, start + c : start + c + step] = best
        return carry

    lax.fori_loop(0, rows // CHUNK, chunk, 0)
    mx[0] = jnp.max(top[...], axis=0, keepdims=True)
    for copy in norm_loads:
        copy.wait()
    norms[m, f] = jnp.zeros_like(norms[m, f])
    norms[m, f, :, : norm_in.shape[2]] = norm_in[0] + norm_in[1]

    pl.semaphore_wait(barrier, 7)

    def remote(src, dst, s, d, peer):
        return pltpu.make_async_remote_copy(
            src_ref=src, dst_ref=dst, send_sem=s, recv_sem=d, device_id=peer, device_id_type=MESH
        )

    small = []
    for k, peer in enumerate(plane):
        copy = remote(mx.at[0], mx.at[1 + k], mx_send.at[k], mx_recv.at[k], peer)
        copy.start()
        small.append(copy)
    tags = []
    for k, peer in enumerate(plane):
        copy = remote(norms.at[m, f], norms.at[m, f], nm_send.at[k], nm_recv.at[k], peer)
        copy.start()
        tags.append(copy)
    ahead = []
    for k in range(2):
        for a in range(3):
            copy = remote(
                fresh[a].at[pl.ds(part_a, rows - part_a)], early[a].at[k],
                early_send.at[k * 3 + a], early_recv.at[k * 3 + a], plane[k],
            )
            copy.start()
            ahead.append(copy)
    for copy in small:
        copy.wait_recv()
    mx[4] = jnp.maximum(jnp.maximum(mx[0], mx[1]), jnp.maximum(mx[2], mx[3]))
    for k, peer in enumerate(line):
        copy = remote(mx.at[4], mx.at[5 + k], mx_send.at[3 + k], mx_recv.at[3 + k], peer)
        copy.start()
        small.append(copy)
    for k, rr in enumerate((rx, ry, rd)):
        mine = norms.at[m, z * 4 + rr]
        remote(mine, mine, nm_send.at[k], nm_recv.at[k], plane[k]).wait_recv()
    group = norms.at[m, pl.ds(z * 4, 4)]
    for k, peer in enumerate(line):
        copy = remote(group, group, nm_send.at[3 + k], nm_recv.at[3 + k], peer)
        copy.start()
        tags.append(copy)
    for copy in small[3:]:
        copy.wait_recv()
    factor[...] = jnp.maximum(jnp.maximum(mx[4], mx[5]), jnp.maximum(mx[6], mx[7]))

    def narrow(refs, skip, block, first, last):
        def body(i, carry):
            at = pl.ds(pl.multiple_of(first + i * ROWS, ROWS), ROWS)
            here = pl.ds(pl.multiple_of(first - skip + i * ROWS, ROWS), ROWS)
            for ref, start, width in zip(refs, starts, widths):
                step = min(512, width)
                for c in range(0, width, step):
                    scale = factor[:, start + c : start + c + step]
                    held[block, at, start + c : start + c + step] = (
                        ref[here, c : c + step] / scale
                    ).astype(jnp.bfloat16)
            return carry
        lax.fori_loop(0, (last - first) // ROWS, body, 0)

    done = []

    def piece(zz, rr, first, last):
        return held.at[zz * 4 + rr, pl.ds(first, last - first)]

    def copy_of(zz, rr, first, last, s, d, peer):
        block = piece(zz, rr, first, last)
        return remote(block, block, send.at[s], recv.at[d], peer)

    def go(make):
        make().start()
        done.append(make)

    def got(zz, rr, first, last, d):
        copy_of(zz, rr, first, last, d, d, plane[0]).wait_recv()

    hi = z // 2
    z_end, z_mid, z_mid2, z_end2 = 3 * hi, 1 + hi, 2 - hi, 3 - 3 * hi
    is_end = z == z_end
    is_mid = z == z_mid
    near = z_end + z_mid - z
    plane_of = (r, rx, ry, rd)

    def az(zz, to, outward):
        go(lambda: copy_of(zz, r, 0, part_a, AZ + zz + (COUNT if outward else 0), AZ + zz, device(to, r)))

    def bz(zz, j, to, outward):
        def make():
            at = BZ + zz * 4 + j
            back = at + (COUNT if outward else 0)
            return copy_of(zz, plane_of[j], part_a, rows, back, at, device(to, r))
        go(make)

    def got_az(zz):
        got(zz, r, 0, part_a, AZ + zz)

    def got_bz(zz, j):
        got(zz, plane_of[j], part_a, rows, BZ + zz * 4 + j)

    def a_own(zz):
        go(lambda: copy_of(zz, r, 0, part_a, AX + zz, AX + zz, plane[0]))
        go(lambda: copy_of(zz, r, 0, part_a, AY + zz, AY + zz, plane[1]))

    def a_forward(zz):
        got(zz, rx, 0, part_a, AX + zz)
        go(lambda: copy_of(zz, rx, half_a, part_a, AYF + zz, AYF + zz, plane[1]))
        got(zz, ry, 0, part_a, AY + zz)
        go(lambda: copy_of(zz, ry, 0, half_a, AXF + zz, AXF + zz, plane[0]))

    narrow(fresh, 0, f, 0, part_a)

    tail = []

    def branch(pred):
        def wrap(body):
            @pl.when(pred)
            def _():
                kept = list(done)
                done.clear()
                body()
                tail.append((pred, list(done)))
                done.clear()
                done.extend(kept)
        return wrap

    @branch(is_end)
    def _():
        az(z_end, z_mid, False)

    @branch(is_mid)
    def _():
        az(z_mid, z_mid2, False)
        az(z_mid, z_end, True)

    a_own(z)
    narrow(fresh, 0, f, part_a, rows)
    for k, rr in enumerate((rx, ry)):
        for copy in ahead[k * 3 : k * 3 + 3]:
            copy.wait_recv()
        narrow([ref.at[k] for ref in early], part_a, z * 4 + rr, part_a, rows)
        if k == 0:
            go(lambda: copy_of(z, rx, part_a + half_b, rows, BYF, BYF, plane[1]))
    go(lambda: copy_of(z, ry, part_a, part_a + half_b, BXF, BXF, plane[0]))

    @branch(is_end)
    def _():
        for j in (0, 1):
            bz(z_end, j, z_mid, False)
        got_az(z_mid)

    @branch(is_mid)
    def _():
        for j in (0, 1):
            bz(z_mid, j, z_mid2, False)
            bz(z_mid, j, z_end, True)
        got_az(z_end)
        az(z_end, z_mid2, False)
        got_az(z_mid2)
        az(z_mid2, z_end, True)

    a_own(near)
    got(z, rd, part_a, part_a + half_b, BXF)
    got(z, rd, part_a + half_b, rows, BYF)

    @branch(is_end)
    def _():
        for j in (2, 3):
            bz(z_end, j, z_mid, False)

    @branch(is_mid)
    def _():
        for j in (2, 3):
            bz(z_mid, j, z_mid2, False)
            bz(z_mid, j, z_end, True)

    a_forward(z)

    @branch(is_end)
    def _():
        got_az(z_mid2)

    a_own(z_mid2)

    @branch(is_mid)
    def _():
        got_az(z_end2)
        az(z_end2, z_end, True)

    a_forward(near)

    @branch(is_mid)
    def _():
        for j in range(4):
            got_bz(z_end, j)
            bz(z_end, j, z_mid2, False)
        for j in range(4):
            got_bz(z_mid2, j)
            bz(z_mid2, j, z_end, True)

    @branch(is_end)
    def _():
        got_az(z_end2)

    a_own(z_end2)
    a_forward(z_mid2)

    @branch(is_mid)
    def _():
        for j in range(4):
            got_bz(z_end2, j)
            bz(z_end2, j, z_end, True)

    for k in range(1, 4):
        theirs = norms.at[m, pl.ds(((z + 4 - k) % 4) * 4, 4)]
        remote(theirs, theirs, nm_send.at[2 + k], nm_recv.at[2 + k], line[k - 1]).wait_recv()
    whole = norms.at[m]
    copy = remote(whole, whole, nm_send.at[6], nm_recv.at[6], partner)
    copy.start()
    tags.append(copy)

    a_forward(z_end2)

    @branch(is_end)
    def _():
        for zz in (z_mid, z_mid2, z_end2):
            for j in range(4):
                got_bz(zz, j)

    for zz in (z, near, z_mid2, z_end2):
        got(zz, rd, 0, half_a, AXF + zz)
        got(zz, rd, half_a, part_a, AYF + zz)
    theirs = norms.at[1 - m]
    remote(theirs, theirs, nm_send.at[6], nm_recv.at[6], partner).wait_recv()
    for copy in small + tags + ahead:
        copy.wait_send()
    for make in done:
        make().wait_send()
    for pred in (is_end, is_mid):
        @pl.when(pred)
        def _(pred=pred):
            for which, copies in tail:
                if which is pred:
                    for make in copies:
                        make().wait_send()


def write_kernel(held, fresh_q, fresh_k, fresh_v, factor, *rest):
    serve, rates, fresh_out, sems = rest[:3], rest[3:6], rest[6:9], rest[9]
    n = held.shape[0]
    cut = max(1, n // 4)
    copies = []
    start = 0
    for k in range(3):
        width = serve[k].shape[2]
        for b in range(0, n, cut):
            copies.append((held.at[pl.ds(b, cut), :, pl.ds(start, width)], serve[k].at[pl.ds(b, cut)]))
        copies.append((factor.at[:, pl.ds(start, width)], rates[k]))
        copies.append(((fresh_q, fresh_k, fresh_v)[k], fresh_out[k]))
        start += width
    copies = [pltpu.make_async_copy(src, dst, sems.at[i]) for i, (src, dst) in enumerate(copies)]
    for copy in copies:
        copy.start()
    for copy in copies:
        copy.wait()


def with_kernel(part_a, *args):
    (tq, dq, sq, tk, dk, sk, tv, dv, sv, norm_train, norm_step) = args
    length = norm_train.shape[0]
    padded = -(-length // LANES) * LANES
    n, cores = lax.axis_size("fsdp"), lax.axis_size("model")
    rows = tq.shape[0]
    widths = (tq.shape[1], tk.shape[1], tv.shape[1])
    width = sum(widths)
    vmem = pl.BlockSpec(memory_space=pltpu.VMEM)
    hbm = pl.BlockSpec(memory_space=pltpu.HBM)
    f32, bf16 = jnp.float32, jnp.bfloat16
    room = VMEM_BYTES - n * rows * width * 2 - rows * width * 4 - 192 * 1024
    held, fresh_q, fresh_k, fresh_v, factor, norms = pl.pallas_call(
        functools.partial(gather_kernel, part_a),
        out_shape=(
            pltpu.VMEM((n, rows, width), bf16),
            *[pltpu.VMEM((rows, w), f32) for w in widths],
            pltpu.VMEM((1, width), f32),
            jax.ShapeDtypeStruct((cores, n, 1, padded), f32),
        ),
        in_specs=[hbm] * 11,
        out_specs=(vmem,) * 6,
        scratch_shapes=[
            *[pltpu.VMEM((3, rows, w), f32) for w in widths],
            pltpu.VMEM((2, 1, length), f32),
            pltpu.VMEM((8, width), f32),
            *[pltpu.VMEM((2, rows - part_a, w), f32) for w in widths],
            pltpu.VMEM((8, 1, width), f32),
            pltpu.SemaphoreType.DMA((rows // CHUNK, 9)),
            pltpu.SemaphoreType.DMA((2,)),
            pltpu.SemaphoreType.DMA((6,)),
            pltpu.SemaphoreType.DMA((6,)),
            pltpu.SemaphoreType.DMA((7,)),
            pltpu.SemaphoreType.DMA((7,)),
            pltpu.SemaphoreType.DMA((6,)),
            pltpu.SemaphoreType.DMA((6,)),
            pltpu.SemaphoreType.DMA((COUNT + AX,)),
            pltpu.SemaphoreType.DMA((COUNT,)),
        ],
        compiler_params=pltpu.CompilerParams(
            collective_id=0, has_side_effects=True, vmem_limit_bytes=room
        ),
        name="gather",
    )(
        tq, dq, sq, tk, dk, sk, tv, dv, sv,
        norm_train.reshape(1, length), norm_step.reshape(1, length),
    )
    out = pl.pallas_call(
        write_kernel,
        out_shape=(
            *[jax.ShapeDtypeStruct((n, rows, w), bf16) for w in widths],
            *[jax.ShapeDtypeStruct((1, w), f32) for w in widths],
            *[jax.ShapeDtypeStruct((rows, w), f32) for w in widths],
        ),
        in_specs=[vmem] * 5,
        out_specs=(hbm,) * 9,
        scratch_shapes=[pltpu.SemaphoreType.DMA((18,))],
        compiler_params=pltpu.CompilerParams(vmem_limit_bytes=4 * 1024 * 1024),
        name="write",
    )(held, fresh_q, fresh_k, fresh_v, factor)
    serve_norm = (
        norms[:, :, 0, :length].transpose(1, 0, 2).reshape(n * cores * length).astype(bf16)
    )
    return (
        *[a.reshape(n * rows, w) for a, w in zip(out[:3], widths)],
        *[a.reshape(w) for a, w in zip(out[3:6], widths)],
        serve_norm, *out[6:],
    )


def per_device(
    train_query,
    drift_query,
    spread_query,
    train_key,
    drift_key,
    spread_key,
    train_value,
    drift_value,
    spread_value,
    norm_train,
    norm_step,
):
    n, cores, rows = lax.axis_size("fsdp"), lax.axis_size("model"), train_query.shape[0]
    part_a = rows - (rows * 2 // 9 // (2 * ROWS)) * 2 * ROWS
    lanes_ok = all(a.shape[1] % LANES == 0 for a in (train_query, train_key, train_value))
    if n == 16 and cores == 2 and rows % CHUNK == 0 and part_a < rows and lanes_ok:
        return with_kernel(
            part_a,
            train_query, drift_query, spread_query,
            train_key, drift_key, spread_key,
            train_value, drift_value, spread_value,
            norm_train, norm_step,
        )
    fresh_query = train_query - learn_rate * (
        drift_query / (jnp.sqrt(spread_query) + tiny_value) + decay_rate * train_query
    )
    fresh_key = train_key - learn_rate * (
        drift_key / (jnp.sqrt(spread_key) + tiny_value) + decay_rate * train_key
    )
    fresh_value = train_value - learn_rate * (
        drift_value / (jnp.sqrt(spread_value) + tiny_value) + decay_rate * train_value
    )
    factor_query, factor_key, factor_value = lax.pmax(
        (
            jnp.max(jnp.abs(fresh_query), axis=0),
            jnp.max(jnp.abs(fresh_key), axis=0),
            jnp.max(jnp.abs(fresh_value), axis=0),
        ),
        "fsdp",
    )
    narrow_query, narrow_key, narrow_value = (
        (fresh_query / factor_query).astype(jnp.bfloat16),
        (fresh_key / factor_key).astype(jnp.bfloat16),
        (fresh_value / factor_value).astype(jnp.bfloat16),
    )
    serve_query, serve_key, serve_value = (
        lax.all_gather(narrow_query, "fsdp", axis=0, tiled=True),
        lax.all_gather(narrow_key, "fsdp", axis=0, tiled=True),
        lax.all_gather(narrow_value, "fsdp", axis=0, tiled=True),
    )
    serve_norm = lax.all_gather(
        (norm_train + norm_step).astype(jnp.bfloat16), ("fsdp", "model"), axis=0, tiled=True
    )
    return (
        serve_query,
        serve_key,
        serve_value,
        factor_query,
        factor_key,
        factor_value,
        serve_norm,
        fresh_query,
        fresh_key,
        fresh_value,
    )


def solution(mesh):
    in_specs = (
        P("fsdp", "model"),
        P("fsdp", "model"),
        P("fsdp", "model"),
        P("fsdp", "model"),
        P("fsdp", "model"),
        P("fsdp", "model"),
        P("fsdp", "model"),
        P("fsdp", "model"),
        P("fsdp", "model"),
        P(("fsdp", "model")),
        P(("fsdp", "model")),
    )
    out_specs = (
        P(None, "model"),
        P(None, "model"),
        P(None, "model"),
        P("model"),
        P("model"),
        P("model"),
        P(),
        P("fsdp", "model"),
        P("fsdp", "model"),
        P("fsdp", "model"),
    )
    return jax.shard_map(
        per_device, mesh=mesh, in_specs=in_specs, out_specs=out_specs, check_vma=False
    )
```

profile of v0, /device:TPU:0, one launch (start us, length us, event | category | flops | bytes accessed | tf_op | source)
XLA Modules:
  0.0 129.2 jit_solution(1660080170916957855)
XLA Ops:
  0.6 121.6 %gather.1 = (bf16[16,160,3072]{2,1,0:T(8,128)(2,1)S(1)}, f32[160,2048]{1,0:T(8,128)S(1)}, f32[160,512]{1,0:T(8,128)S(1)}, f32[160,512]{1,0:T(8,128)S(1)}, f32[1,...) custom-call(f32[160,2048]{1,0:T(8,128)} %tq.1, f32[160,2048]{1,0:T(8,128)} %dq.1, f32[160,2048]{1,0:T(8,128)} %sq.1, ...), custom_call_target="tpu_custom_call" | custom-call | tf_op jit(solution)/shard_map/gather/pallas_call | solution.py:382
  122.2 0.0 copy-start
  122.2 6.3 %write.1 = (bf16[16,160,2048]{2,1,0:T(8,128)(2,1)}, bf16[16,160,512]{2,1,0:T(8,128)(2,1)}, bf16[16,160,512]{2,1,0:T(8,128)(2,1)}, f32[1,2048]{1,0:T(1,128)}, f32...) custom-call(bf16[16,160,3072]{2,1,0:T(8,128)(2,1)S(1)} %get-tuple-elemen, ...), custom_call_target="tpu_custom_call" | custom-call | tf_op jit(solution)/shard_map/write/pallas_call | solution.py:417
  128.5 0.0 copy-done
  128.6 0.7 convert_element_type.12
  (3 shorter events, 0.0 us)
Async XLA Ops:
  122.2 6.3 %copy-start = (f32[2,16,1,128]{3,2,1,0:T(1,128)S(1)}, f32[2,16,1,128]{3,2,1,0:T(1,128)}, u32[]{:S(2)}) copy-start(f32[2,16,1,128]{3,2,1,0:T(1,128)} %get-tuple-element.36) | copy-start | bytes 49156
where the time goes:
time: 129 us
  Pallas kernels  128 us (99%)
    pallas_call x1, Pallas kernels, with_kernel(): pl.pallas_call(functools.partial(gather_kernel, part_a), out_shape=(pltpu...  122 us
    pallas_call x1, Pallas kernels, with_kernel(): pl.pallas_call(write_kernel, out_shape=(*[jax.ShapeDtypeStruct((n, rows,...  6.27 us

commit v1 on v0

v1 whole, which is shorter than its diff:
```python
import functools
import math

import jax
import jax.numpy as jnp
from jax import lax
from jax.experimental import pallas as pl
from jax.experimental.pallas import tpu as pltpu
from jax.sharding import PartitionSpec as P

learn_rate = 0.02
decay_rate = 0.05
tiny_value = 1e-08
MESH = pl.DeviceIdType.MESH
ROWS = 16
CHUNK = 32
VMEM_BYTES = 67043328
LANES = 128

AZ, BZ, AX, AY, BXF, BYF, DIAG, COUNT = 0, 4, 20, 24, 28, 29, 30, 31
TO_X, TO_Y, INWARD, OUTWARD = 0, 1, 2, 3


def stepped(train, drift, spread):
    return train - learn_rate * (drift / (jnp.sqrt(spread) + tiny_value) + decay_rate * train)


def gather_kernel(
    part_a, widths,
    tq, dq, sq, tk, dk, sk, tv, dv, sv, norm_train, norm_step,
    held, fresh, factor, norms,
    local, norm_in, top, early,
    mx, in_sem, norm_sem, mx_send, mx_recv, nm_send, nm_recv, early_send, early_recv, send, recv,
):
    f = lax.axis_index("fsdp")
    m = lax.axis_index("model")
    z = f // 4
    r = f % 4
    y = r // 2
    x = r % 2
    rx, ry, rd = y * 2 + (1 - x), (1 - y) * 2 + x, (1 - y) * 2 + (1 - x)
    n, rows, width = held.shape
    starts = (0, widths[0], widths[0] + widths[1])
    inputs = ((tq, dq, sq), (tk, dk, sk), (tv, dv, sv))
    half_a = part_a // 2
    half_b = (rows - part_a) // 2

    def device(zz, rr):
        return {"fsdp": zz * 4 + rr, "model": m}

    plane = [device(z, rx), device(z, ry), device(z, rd)]
    line = [device((z + k) % 4, r) for k in range(1, 4)]
    partner = {"fsdp": f, "model": 1 - m}

    barrier = pltpu.get_barrier_semaphore()
    for peer in plane + line + [partner]:
        pl.semaphore_signal(barrier, inc=1, device_id=peer, device_id_type=MESH)

    def part(i):
        return pl.ds(pl.multiple_of(i * CHUNK, CHUNK), CHUNK)

    for i in range(rows // CHUNK):
        for a in range(3):
            cols = pl.ds(starts[a], widths[a])
            for k, src in enumerate(inputs[a]):
                pltpu.make_async_copy(src.at[part(i)], local.at[k, part(i), cols], in_sem.at[i]).start()
    norm_loads = [
        pltpu.make_async_copy(src, norm_in.at[k], norm_sem.at[k])
        for k, src in enumerate((norm_train, norm_step))
    ]
    for copy in norm_loads:
        copy.start()

    top[...] = jnp.zeros_like(top)
    step = math.gcd(512, width)

    def chunk(i, carry):
        whole = local.at[:, part(i)]
        pltpu.make_async_copy(whole, whole, in_sem.at[i]).wait()
        for c in range(0, width, step):
            cols = slice(c, c + step)
            best = top[:, cols]
            for g in range(CHUNK // 8):
                at = pl.ds(pl.multiple_of(i * CHUNK + g * 8, 8), 8)
                new = stepped(local[0, at, cols], local[1, at, cols], local[2, at, cols])
                fresh[at, cols] = new
                best = jnp.maximum(best, jnp.abs(new))
            top[:, cols] = best
        return carry

    lax.fori_loop(0, rows // CHUNK, chunk, 0)
    mx[0] = jnp.max(top[...], axis=0, keepdims=True)
    for copy in norm_loads:
        copy.wait()
    norms[m, f] = jnp.zeros_like(norms[m, f])
    norms[m, f, :, : norm_in.shape[2]] = norm_in[0] + norm_in[1]

    pl.semaphore_wait(barrier, 7)

    def remote(src, dst, s, d, peer):
        return pltpu.make_async_remote_copy(
            src_ref=src, dst_ref=dst, send_sem=s, recv_sem=d, device_id=peer, device_id_type=MESH
        )

    for k, peer in enumerate(plane):
        remote(mx.at[0], mx.at[1 + k], mx_send.at[0], mx_recv.at[0], peer).start()
    mine = norms.at[m, f]
    for peer in plane:
        remote(mine, mine, nm_send.at[0], nm_recv.at[0], peer).start()
    for k in range(2):
        remote(fresh.at[pl.ds(part_a, rows - part_a)], early.at[k], early_send.at[0], early_recv.at[k], plane[k]).start()
    got_mx = mx.at[pl.ds(1, 3)]
    remote(got_mx, got_mx, mx_send.at[0], mx_recv.at[0], plane[0]).wait_recv()
    mx[4] = jnp.maximum(jnp.maximum(mx[0], mx[1]), jnp.maximum(mx[2], mx[3]))
    for k, peer in enumerate(line):
        remote(mx.at[4], mx.at[5 + k], mx_send.at[0], mx_recv.at[1], peer).start()
    got_nm = norms.at[m, pl.ds(0, 3)]
    remote(got_nm, got_nm, nm_send.at[0], nm_recv.at[0], plane[0]).wait_recv()
    group = norms.at[m, pl.ds(z * 4, 4)]
    for peer in line:
        remote(group, group, nm_send.at[0], nm_recv.at[1], peer).start()
    remote(got_mx, got_mx, mx_send.at[0], mx_recv.at[1], plane[0]).wait_recv()
    factor[...] = jnp.maximum(jnp.maximum(mx[4], mx[5]), jnp.maximum(mx[6], mx[7]))

    def narrow(ref, skip, block, first, last):
        def body(i, carry):
            at = pl.ds(pl.multiple_of(first + i * ROWS, ROWS), ROWS)
            here = pl.ds(pl.multiple_of(first - skip + i * ROWS, ROWS), ROWS)
            for c in range(0, width, step):
                cols = slice(c, c + step)
                held[block, at, cols] = (ref[here, cols] / factor[:, cols]).astype(jnp.bfloat16)
            return carry
        lax.fori_loop(0, (last - first) // ROWS, body, 0)

    def go(zz, rr, first, last, way, d, peer):
        block = held.at[zz * 4 + rr, pl.ds(first, last - first)]
        remote(block, block, send.at[way], recv.at[d], peer).start()

    def got(zz, rr, first, last, d):
        block = held.at[zz * 4 + rr, pl.ds(first, last - first)]
        remote(block, block, send.at[0], recv.at[d], plane[0]).wait_recv()

    def span(count):
        for blocks in range(1, n + 1):
            if count % (blocks * 8) == 0 and count // blocks <= rows:
                return held.at[pl.ds(0, blocks), pl.ds(0, count // blocks)]
        raise ValueError(count)

    def sent(way, count):
        all_of = span(count)
        remote(all_of, all_of, send.at[way], recv.at[0], plane[0]).wait_send()

    hi = z // 2
    z_end, z_mid, z_mid2, z_end2 = 3 * hi, 1 + hi, 2 - hi, 3 - 3 * hi
    is_end = z == z_end
    is_mid = z == z_mid
    near = z_end + z_mid - z
    plane_of = (r, rx, ry, rd)

    def az(zz, to, outward):
        go(zz, r, 0, part_a, OUTWARD if outward else INWARD, AZ + zz, device(to, r))

    def bz(zz, j, to, outward):
        go(zz, plane_of[j], part_a, rows, OUTWARD if outward else INWARD, BZ + zz * 4 + j, device(to, r))

    def got_az(zz):
        got(zz, r, 0, part_a, AZ + zz)

    def got_bz(zz, j):
        got(zz, plane_of[j], part_a, rows, BZ + zz * 4 + j)

    def a_own(zz):
        go(zz, r, 0, part_a, TO_X, AX + zz, plane[0])
        go(zz, r, 0, part_a, TO_Y, AY + zz, plane[1])

    def a_forward(zz):
        got(zz, rx, 0, part_a, AX + zz)
        go(zz, rx, half_a, part_a, TO_Y, DIAG, plane[1])
        got(zz, ry, 0, part_a, AY + zz)
        go(zz, ry, 0, half_a, TO_X, DIAG, plane[0])

    narrow(fresh, 0, f, 0, part_a)

    @pl.when(is_end)
    def _():
        az(z_end, z_mid, False)

    @pl.when(is_mid)
    def _():
        az(z_mid, z_mid2, False)
        az(z_mid, z_end, True)

    a_own(z)
    narrow(fresh, 0, f, part_a, rows)
    for k, rr in enumerate((rx, ry)):
        remote(early.at[k], early.at[k], early_send.at[0], early_recv.at[k], plane[k]).wait_recv()
        narrow(early.at[k], part_a, z * 4 + rr, part_a, rows)
        if k == 0:
            go(z, rx, part_a + half_b, rows, TO_Y, BYF, plane[1])
    go(z, ry, part_a, part_a + half_b, TO_X, BXF, plane[0])

    @pl.when(is_end)
    def _():
        for j in (0, 1):
            bz(z_end, j, z_mid, False)
        got_az(z_mid)

    @pl.when(is_mid)
    def _():
        for j in (0, 1):
            bz(z_mid, j, z_mid2, False)
            bz(z_mid, j, z_end, True)
        got_az(z_end)
        az(z_end, z_mid2, False)
        got_az(z_mid2)
        az(z_mid2, z_end, True)

    a_own(near)
    got(z, rd, part_a, part_a + half_b, BXF)
    got(z, rd, part_a + half_b, rows, BYF)

    @pl.when(is_end)
    def _():
        for j in (2, 3):
            bz(z_end, j, z_mid, False)

    @pl.when(is_mid)
    def _():
        for j in (2, 3):
            bz(z_mid, j, z_mid2, False)
            bz(z_mid, j, z_end, True)

    a_forward(z)

    @pl.when(is_end)
    def _():
        got_az(z_mid2)

    a_own(z_mid2)

    @pl.when(is_mid)
    def _():
        got_az(z_end2)
        az(z_end2, z_end, True)

    a_forward(near)

    @pl.when(is_mid)
    def _():
        for j in range(4):
            got_bz(z_end, j)
            bz(z_end, j, z_mid2, False)
        for j in range(4):
            got_bz(z_mid2, j)
            bz(z_mid2, j, z_end, True)

    @pl.when(is_end)
    def _():
        got_az(z_end2)

    a_own(z_end2)
    a_forward(z_mid2)

    @pl.when(is_mid)
    def _():
        for j in range(4):
            got_bz(z_end2, j)
            bz(z_end2, j, z_end, True)

    got_nm = norms.at[m, pl.ds(0, 12)]
    remote(got_nm, got_nm, nm_send.at[0], nm_recv.at[1], plane[0]).wait_recv()
    whole = norms.at[m]
    remote(whole, whole, nm_send.at[1], nm_recv.at[2], partner).start()

    a_forward(z_end2)

    @pl.when(is_end)
    def _():
        for zz in (z_mid, z_mid2, z_end2):
            for j in range(4):
                got_bz(zz, j)

    diagonal = span(4 * part_a)
    remote(diagonal, diagonal, send.at[0], recv.at[DIAG], plane[0]).wait_recv()
    theirs = norms.at[1 - m]
    remote(theirs, theirs, nm_send.at[1], nm_recv.at[2], partner).wait_recv()
    sums = mx.at[pl.ds(0, 6)]
    remote(sums, sums, mx_send.at[0], mx_recv.at[0], plane[0]).wait_send()
    tags = norms.at[m, pl.ds(0, 15)]
    remote(tags, tags, nm_send.at[0], nm_recv.at[0], plane[0]).wait_send()
    remote(theirs, theirs, nm_send.at[1], nm_recv.at[2], partner).wait_send()
    remote(early, early, early_send.at[0], early_recv.at[0], plane[0]).wait_send()
    sent(TO_X, 4 * (part_a + half_a) + half_b)
    sent(TO_Y, 4 * (part_a + part_a - half_a) + rows - part_a - half_b)
    up = part_a + 4 * (rows - part_a)

    @pl.when(is_end)
    def _():
        sent(INWARD, up)

    @pl.when(is_mid)
    def _():
        sent(INWARD, 2 * up)
        sent(OUTWARD, 3 * up)


def write_kernel(length, held, fresh, factor, norms, *rest):
    serve, rates, fresh_out, norm_out, flat, norm_row, sems = rest[:3], rest[3:6], rest[6:9], *rest[9:]
    n = held.shape[0]
    cut = max(1, n // 4)
    copies = []
    start = 0
    for k in range(3):
        cols = pl.ds(start, serve[k].shape[2])
        for b in range(0, n, cut):
            copies.append((held.at[pl.ds(b, cut), :, cols], serve[k].at[pl.ds(b, cut)]))
        copies.append((factor.at[:, cols], rates[k]))
        copies.append((fresh.at[:, cols], fresh_out[k]))
        start += serve[k].shape[2]
    copies = [pltpu.make_async_copy(src, dst, sems.at[i]) for i, (src, dst) in enumerate(copies)]
    for copy in copies:
        copy.start()
    at = 0
    for b in range(n):
        for c in range(norms.shape[0]):
            flat[:, at : at + length] = norms[c, b, :, :length]
            at += length
    norm_row[...] = flat[...].astype(jnp.bfloat16).reshape(at)
    last = pltpu.make_async_copy(norm_row, norm_out, sems.at[len(copies)])
    last.start()
    for copy in copies:
        copy.wait()
    last.wait()


def with_kernel(part_a, *args):
    (tq, dq, sq, tk, dk, sk, tv, dv, sv, norm_train, norm_step) = args
    length = norm_train.shape[0]
    padded = -(-length // LANES) * LANES
    n, cores = lax.axis_size("fsdp"), lax.axis_size("model")
    rows = tq.shape[0]
    widths = (tq.shape[1], tk.shape[1], tv.shape[1])
    width = sum(widths)
    vmem = pl.BlockSpec(memory_space=pltpu.VMEM)
    hbm = pl.BlockSpec(memory_space=pltpu.HBM)
    f32, bf16 = jnp.float32, jnp.bfloat16
    room = VMEM_BYTES - n * rows * width * 2 - rows * width * 4 - 192 * 1024
    held, fresh, factor, norms = pl.pallas_call(
        functools.partial(gather_kernel, part_a, widths),
        out_shape=(
            pltpu.VMEM((n, rows, width), bf16),
            pltpu.VMEM((rows, width), f32),
            pltpu.VMEM((1, width), f32),
            pltpu.VMEM((cores, n, 1, padded), f32),
        ),
        in_specs=[hbm] * 11,
        out_specs=(vmem,) * 4,
        scratch_shapes=[
            pltpu.VMEM((3, rows, width), f32),
            pltpu.VMEM((2, 1, length), f32),
            pltpu.VMEM((8, width), f32),
            pltpu.VMEM((2, rows - part_a, width), f32),
            pltpu.VMEM((8, 1, width), f32),
            pltpu.SemaphoreType.DMA((rows // CHUNK,)),
            pltpu.SemaphoreType.DMA((2,)),
            pltpu.SemaphoreType.DMA((1,)),
            pltpu.SemaphoreType.DMA((2,)),
            pltpu.SemaphoreType.DMA((2,)),
            pltpu.SemaphoreType.DMA((3,)),
            pltpu.SemaphoreType.DMA((1,)),
            pltpu.SemaphoreType.DMA((2,)),
            pltpu.SemaphoreType.DMA((4,)),
            pltpu.SemaphoreType.DMA((COUNT,)),
        ],
        compiler_params=pltpu.CompilerParams(
            collective_id=0, has_side_effects=True, vmem_limit_bytes=room
        ),
        name="gather",
    )(
        tq, dq, sq, tk, dk, sk, tv, dv, sv,
        norm_train.reshape(1, length), norm_step.reshape(1, length),
    )
    out = pl.pallas_call(
        functools.partial(write_kernel, length),
        out_shape=(
            *[jax.ShapeDtypeStruct((n, rows, w), bf16) for w in widths],
            *[jax.ShapeDtypeStruct((1, w), f32) for w in widths],
            *[jax.ShapeDtypeStruct((rows, w), f32) for w in widths],
            jax.ShapeDtypeStruct((n * cores * length,), bf16),
        ),
        in_specs=[vmem] * 4,
        out_specs=(hbm,) * 10,
        scratch_shapes=[
            pltpu.VMEM((1, n * cores * length), f32),
            pltpu.VMEM((n * cores * length,), bf16),
            pltpu.SemaphoreType.DMA((19,)),
        ],
        compiler_params=pltpu.CompilerParams(vmem_limit_bytes=4 * 1024 * 1024),
        name="write",
    )(held, fresh, factor, norms)
    return (
        *[a.reshape(n * rows, w) for a, w in zip(out[:3], widths)],
        *[a.reshape(w) for a, w in zip(out[3:6], widths)],
        out[9], *out[6:9],
    )


def per_device(
    train_query,
    drift_query,
    spread_query,
    train_key,
    drift_key,
    spread_key,
    train_value,
    drift_value,
    spread_value,
    norm_train,
    norm_step,
):
    n, cores, rows = lax.axis_size("fsdp"), lax.axis_size("model"), train_query.shape[0]
    part_a = rows - (rows * 2 // 9 // (2 * ROWS)) * 2 * ROWS
    lanes_ok = all(a.shape[1] % LANES == 0 for a in (train_query, train_key, train_value))
    if n == 16 and cores == 2 and rows % CHUNK == 0 and part_a < rows and lanes_ok:
        return with_kernel(
            part_a,
            train_query, drift_query, spread_query,
            train_key, drift_key, spread_key,
            train_value, drift_value, spread_value,
            norm_train, norm_step,
        )
    fresh_query = train_query - learn_rate * (
        drift_query / (jnp.sqrt(spread_query) + tiny_value) + decay_rate * train_query
    )
    fresh_key = train_key - learn_rate * (
        drift_key / (jnp.sqrt(spread_key) + tiny_value) + decay_rate * train_key
    )
    fresh_value = train_value - learn_rate * (
        drift_value / (jnp.sqrt(spread_value) + tiny_value) + decay_rate * train_value
    )
    factor_query, factor_key, factor_value = lax.pmax(
        (
            jnp.max(jnp.abs(fresh_query), axis=0),
            jnp.max(jnp.abs(fresh_key), axis=0),
            jnp.max(jnp.abs(fresh_value), axis=0),
        ),
        "fsdp",
    )
    narrow_query, narrow_key, narrow_value = (
        (fresh_query / factor_query).astype(jnp.bfloat16),
        (fresh_key / factor_key).astype(jnp.bfloat16),
        (fresh_value / factor_value).astype(jnp.bfloat16),
    )
    serve_query, serve_key, serve_value = (
        lax.all_gather(narrow_query, "fsdp", axis=0, tiled=True),
        lax.all_gather(narrow_key, "fsdp", axis=0, tiled=True),
        lax.all_gather(narrow_value, "fsdp", axis=0, tiled=True),
    )
    serve_norm = lax.all_gather(
        (norm_train + norm_step).astype(jnp.bfloat16), ("fsdp", "model"), axis=0, tiled=True
    )
    return (
        serve_query,
        serve_key,
        serve_value,
        factor_query,
        factor_key,
        factor_value,
        serve_norm,
        fresh_query,
        fresh_key,
        fresh_value,
    )


def solution(mesh):
    in_specs = (
        P("fsdp", "model"),
        P("fsdp", "model"),
        P("fsdp", "model"),
        P("fsdp", "model"),
        P("fsdp", "model"),
        P("fsdp", "model"),
        P("fsdp", "model"),
        P("fsdp", "model"),
        P("fsdp", "model"),
        P(("fsdp", "model")),
        P(("fsdp", "model")),
    )
    out_specs = (
        P(None, "model"),
        P(None, "model"),
        P(None, "model"),
        P("model"),
        P("model"),
        P("model"),
        P(),
        P("fsdp", "model"),
        P("fsdp", "model"),
        P("fsdp", "model"),
    )
    return jax.shard_map(
        per_device, mesh=mesh, in_specs=in_specs, out_specs=out_specs, check_vma=False
    )
```

time: 129 us -> 127 us (0.984)
  Pallas kernels: 128 us -> 126 us
    pallas_call x2, Pallas kernels: 128 us -> 126 us  [the longest x1 120 us: with_kernel(): pl.pallas_call(functools.partial(gather_kernel, part_a, widths), out_shap...]
where the time goes in v1:
time: 127 us
  Pallas kernels  126 us (99%)
    pallas_call x1, Pallas kernels, with_kernel(): pl.pallas_call(functools.partial(gather_kernel, part_a, widths), out_shap...  120 us
    pallas_call x1, Pallas kernels, with_kernel(): pl.pallas_call(functools.partial(write_kernel, length), out_shape=(*[jax....  6.28 us

profile of v1, /device:TPU:0, one launch (start us, length us, event | category | flops | bytes accessed | tf_op | source)
XLA Modules:
  0.0 126.7 jit_solution(3572080407133062528)
XLA Ops:
  0.6 119.7 %gather.1 = (bf16[16,160,3072]{2,1,0:T(8,128)(2,1)S(1)}, f32[160,3072]{1,0:T(8,128)S(1)}, f32[1,3072]{1,0:T(1,128)S(1)}, f32[2,16,1,128]{3,2,1,0:T(1,128)S(1)}) custom-call(f32[160,2048]{1,0:T(8,128)} %tq.1, f32[160,2048]{1,0:T(8,128)} %dq.1, f32[160,2048]{1,0:T(8,128)} %sq.1, f32[160,512]{1,0:T(8,128)} %tk.1, f32[160,512]{1,0:T(8,128)} %dk.1, ...), custom_call_target="tpu_custom_call" | custom-call | tf_op jit(solution)/shard_map/gather/pallas_call | solution.py:348
  120.4 6.3 %write.1 = (bf16[16,160,2048]{2,1,0:T(8,128)(2,1)}, bf16[16,160,512]{2,1,0:T(8,128)(2,1)}, bf16[16,160,512]{2,1,0:T(8,128)(2,1)}, f32[1,2048]{1,0:T(1,128)}, f32...) custom-call(bf16[16,160,3072]{2,1,0:T(8,128)(2,1)S(1)} %get-tuple-el, ...), custom_call_target="tpu_custom_call" | custom-call | tf_op jit(solution)/shard_map/write/pallas_call | solution.py:383

commit v2 on v1

v2 whole, which is shorter than its diff:
```python
import functools
import math

import jax
import jax.numpy as jnp
from jax import lax
from jax.experimental import pallas as pl
from jax.experimental.pallas import tpu as pltpu
from jax.sharding import PartitionSpec as P

learn_rate = 0.02
decay_rate = 0.05
tiny_value = 1e-08
MESH = pl.DeviceIdType.MESH
ROWS = 8
SUB = 8
CHUNK = 32
VMEM_BYTES = 67043328
LANES = 128

AZ, BZ, AX, AY, BXF, BYF, DIAG, BX, BY, COUNT = 0, 4, 20, 24, 28, 29, 30, 31, 32, 33
EARLY, FIRST, LEAD = 16, 8, 6
AX_SENT, AY_SENT, FX_SENT, FY_SENT, BX_SENT, BY_SENT, IN_A, IN_B, OUT_A, OUT_B, KINDS = range(11)


def stepped(train, drift, spread):
    return train - learn_rate * (drift / (jnp.sqrt(spread) + tiny_value) + decay_rate * train)


def cover(count, blocks, down, across):
    for c in range(across, 0, -1):
        for b in range(1, blocks + 1):
            if count % (b * c) == 0 and count // (b * c) <= down:
                return b, count // (b * c), c
    raise ValueError("no cover")


def gather_kernel(
    part_a, split, widths,
    tq, dq, sq, tk, dk, sk, tv, dv, sv, norm_train, norm_step,
    held, fresh, factor, norms,
    local, norm_in, top, early,
    mx, lead_sem, in_sem, norm_sem, mx_send, mx_recv, nm_send, nm_recv, early_send, early_recv, send, recv,
):
    f = lax.axis_index("fsdp")
    m = lax.axis_index("model")
    z = f // 4
    r = f % 4
    y = r // 2
    x = r % 2
    rx, ry, rd = y * 2 + (1 - x), (1 - y) * 2 + x, (1 - y) * 2 + (1 - x)
    n, rows, width = held.shape
    starts = (0, widths[0], widths[0] + widths[1])
    inputs = ((tq, dq, sq), (tk, dk, sk), (tv, dv, sv))
    low, high = part_a

    def device(zz, rr):
        return {"fsdp": zz * 4 + rr, "model": m}

    plane = [device(z, rx), device(z, ry), device(z, rd)]
    line = [device((z + k) % 4, r) for k in range(1, 4)]
    partner = {"fsdp": f, "model": 1 - m}

    barrier = pltpu.get_barrier_semaphore()
    for peer in plane + line + [partner]:
        pl.semaphore_signal(barrier, inc=1, device_id=peer, device_id_type=MESH)

    def part(i):
        return pl.ds(pl.multiple_of(i * CHUNK, CHUNK), CHUNK)

    lead, rest = pl.ds(0, split), pl.ds(split, width - split)
    last = rows // CHUNK - 1
    for k, src in enumerate(inputs[0]):
        pltpu.make_async_copy(src.at[:, lead], local.at[k, :, lead], lead_sem.at[0]).start()
    for i in (last, *range(last)):
        for a in range(3):
            skip = split if a == 0 else 0
            here = pl.ds(skip, widths[a] - skip)
            there = pl.ds(starts[a] + skip, widths[a] - skip)
            for k, src in enumerate(inputs[a]):
                pltpu.make_async_copy(src.at[part(i), here], local.at[k, part(i), there], in_sem.at[i]).start()
    norm_loads = [
        pltpu.make_async_copy(src, norm_in.at[k], norm_sem.at[k])
        for k, src in enumerate((norm_train, norm_step))
    ]
    for copy in norm_loads:
        copy.start()

    top[...] = jnp.zeros_like(top)
    step = math.gcd(math.gcd(512, split), width - split)

    def compute(i, low, high):
        for c in range(low, high, step):
            cols = slice(c, c + step)
            best = top[:, cols]
            for g in range(CHUNK // 8):
                at = pl.ds(pl.multiple_of(i * CHUNK + g * 8, 8), 8)
                new = stepped(local[0, at, cols], local[1, at, cols], local[2, at, cols])
                fresh[at, cols] = new
                best = jnp.maximum(best, jnp.abs(new))
            top[:, cols] = best

    def lead_chunk(i, carry):
        compute(i, 0, split)
        return carry

    def chunk(i, carry):
        whole = local.at[:, part(i), rest]
        pltpu.make_async_copy(whole, whole, in_sem.at[i]).wait()
        compute(i, split, width)
        return carry

    whole = local.at[:, :, lead]
    pltpu.make_async_copy(whole, whole, lead_sem.at[0]).wait()
    lax.fori_loop(0, rows // CHUNK, lead_chunk, 0)
    mx[0, :, :split] = jnp.max(top[:, :split], axis=0, keepdims=True)

    pl.semaphore_wait(barrier, 7)

    def remote(src, dst, s, d, peer):
        return pltpu.make_async_remote_copy(
            src_ref=src, dst_ref=dst, send_sem=s, recv_sem=d, device_id=peer, device_id_type=MESH
        )

    def spread(source, first, peers, cols, d):
        for k, peer in enumerate(peers):
            remote(
                mx.at[source, :, cols], mx.at[first + k, :, cols], mx_send.at[0], mx_recv.at[d], peer
            ).start()

    def gathered(cols, d):
        three = mx.at[pl.ds(1, 3), :, cols]
        remote(three, three, mx_send.at[0], mx_recv.at[d], plane[0]).wait_recv()

    def ahead(first, last):
        at = pl.ds(first, last - first)
        to = pl.ds(first - (rows - EARLY), last - first)
        for k in range(2):
            remote(fresh.at[at], early.at[k, to], early_send.at[0], early_recv.at[k], plane[k]).start()

    def plane_max(cols):
        mx[4, :, cols] = jnp.maximum(
            jnp.maximum(mx[0, :, cols], mx[1, :, cols]), jnp.maximum(mx[2, :, cols], mx[3, :, cols])
        )

    def line_max(cols):
        factor[:, cols] = jnp.maximum(
            jnp.maximum(mx[4, :, cols], mx[5, :, cols]), jnp.maximum(mx[6, :, cols], mx[7, :, cols])
        )

    spread(0, 1, plane, lead, 0)
    chunk(last, 0)
    ahead(rows - EARLY, rows - EARLY + FIRST)
    lax.fori_loop(0, last, chunk, 0)
    mx[0, :, split:] = jnp.max(top[:, split:], axis=0, keepdims=True)
    spread(0, 1, plane, rest, 1)
    for copy in norm_loads:
        copy.wait()
    norms[m, f] = jnp.zeros_like(norms[m, f])
    norms[m, f, :, : norm_in.shape[2]] = norm_in[0] + norm_in[1]
    mine = norms.at[m, f]
    for peer in plane:
        remote(mine, mine, nm_send.at[0], nm_recv.at[0], peer).start()
    if FIRST < EARLY:
        ahead(rows - EARLY + FIRST, rows)
    gathered(lead, 0)
    plane_max(slice(0, split))
    spread(4, 5, line, lead, 2)
    gathered(rest, 1)
    plane_max(slice(split, width))
    spread(4, 5, line, rest, 3)
    got_nm = norms.at[m, pl.ds(0, 3)]
    remote(got_nm, got_nm, nm_send.at[0], nm_recv.at[0], plane[0]).wait_recv()
    group = norms.at[m, pl.ds(z * 4, 4)]
    for peer in line:
        remote(group, group, nm_send.at[0], nm_recv.at[1], peer).start()
    gathered(lead, 2)
    line_max(slice(0, split))

    def narrow(ref, skip, block, first, last, low=0, high=width):
        def body(i, carry):
            at = pl.ds(pl.multiple_of(first + i * ROWS, ROWS), ROWS)
            here = pl.ds(pl.multiple_of(first - skip + i * ROWS, ROWS), ROWS)
            for c in range(low, high, step):
                cols = slice(c, c + step)
                held[block, at, cols] = (ref[here, cols] / factor[:, cols]).astype(jnp.bfloat16)
            return carry
        lax.fori_loop(0, (last - first) // ROWS, body, 0)

    def go(zz, rr, piece, way, d, peer):
        for first, last, cols in piece:
            block = held.at[zz * 4 + rr, pl.ds(first, last - first), cols]
            remote(block, block, send.at[way], recv.at[d], peer).start()

    def tiles(piece):
        return sum((last - first) // SUB * (cols.size // LANES) for first, last, cols in piece)

    def span(count):
        blocks, down, across = cover(count, n, rows // SUB, width // LANES)
        return held.at[pl.ds(0, blocks), pl.ds(0, down * SUB), pl.ds(0, across * LANES)]

    def got(piece, d, times=1):
        block = span(tiles(piece) * times)
        remote(block, block, send.at[0], recv.at[d], plane[0]).wait_recv()

    def sent(way, count):
        block = span(count)
        remote(block, block, send.at[way], recv.at[0], plane[0]).wait_send()

    def both(first, last):
        return tuple((p, q, c) for p, q, c in zip(first, last, (lead, rest)) if p < q)

    zero, full, late = (0, 0), (rows, rows), (rows - EARLY, rows - EARLY)
    half_a = tuple(tuple((p + e * SUB) // (2 * SUB) * SUB for p in part_a) for e in (0, 1))
    half_b = tuple(p + (rows - p) // (2 * SUB) * SUB for p in part_a)
    piece_a, piece_b, tail_b = both(zero, part_a), both(part_a, full), both(part_a, late)
    for_x = tuple(both(zero, h) for h in half_a)
    for_y = tuple(both(h, part_a) for h in half_a)
    b_for_x, b_for_y = both(part_a, half_b), both(half_b, full)

    hi = z // 2
    z_end, z_mid, z_mid2, z_end2 = 3 * hi, 1 + hi, 2 - hi, 3 - 3 * hi
    is_end = z == z_end
    is_mid = z == z_mid
    near = z_end + z_mid - z
    plane_of = (r, rx, ry, rd)

    def az(zz, to, outward, piece=piece_a):
        go(zz, r, piece, OUT_A if outward else IN_A, AZ + zz, device(to, r))

    def bz(zz, j, to, outward):
        go(zz, plane_of[j], piece_b, OUT_B if outward else IN_B, BZ + zz * 4 + j, device(to, r))

    def got_az(zz):
        got(piece_a, AZ + zz)

    def got_bz(zz, j):
        got(piece_b, BZ + zz * 4 + j)

    def a_own(zz, piece=piece_a):
        go(zz, r, piece, AX_SENT, AX + zz, plane[0])
        go(zz, r, piece, AY_SENT, AY + zz, plane[1])

    def a_forward(zz, odd):
        got(piece_a, AX + zz)
        go(zz, rx, for_y[odd], FY_SENT, DIAG, plane[1])
        got(piece_a, AY + zz)
        go(zz, ry, for_x[odd], FX_SENT, DIAG, plane[0])

    def outset(piece):
        @pl.when(is_end)
        def _():
            az(z_end, z_mid, False, piece)

        @pl.when(is_mid)
        def _():
            az(z_mid, z_mid2, False, piece)
            az(z_mid, z_end, True, piece)

    narrow(fresh, 0, f, 0, low, 0, split)
    outset(piece_a[:1])
    a_own(z, piece_a[:1])
    gathered(rest, 3)
    line_max(slice(split, width))
    narrow(fresh, 0, f, 0, high, split, width)
    outset(piece_a[1:])
    narrow(fresh, 0, f, low, rows, 0, split)
    narrow(fresh, 0, f, high, rows, split, width)
    if tail_b:
        go(z, r, tail_b, BX_SENT, BX, plane[0])
        go(z, r, tail_b, BY_SENT, BY, plane[1])
    a_own(z, piece_a[1:])
    for k, rr in enumerate((rx, ry)):
        remote(early.at[k], early.at[k], early_send.at[0], early_recv.at[k], plane[k]).wait_recv()
        narrow(early.at[k], rows - EARLY, z * 4 + rr, rows - EARLY, rows)
    if tail_b:
        got(tail_b, BX)
        got(tail_b, BY)
    go(z, rx, b_for_y, BY_SENT, BYF, plane[1])
    go(z, ry, b_for_x, BX_SENT, BXF, plane[0])

    @pl.when(is_end)
    def _():
        for j in (0, 1):
            bz(z_end, j, z_mid, False)
        got_az(z_mid)

    @pl.when(is_mid)
    def _():
        for j in (0, 1):
            bz(z_mid, j, z_mid2, False)
            bz(z_mid, j, z_end, True)
        got_az(z_end)
        az(z_end, z_mid2, False)
        got_az(z_mid2)
        az(z_mid2, z_end, True)

    a_own(near)
    got(b_for_x, BXF)
    got(b_for_y, BYF)

    @pl.when(is_end)
    def _():
        for j in (2, 3):
            bz(z_end, j, z_mid, False)

    @pl.when(is_mid)
    def _():
        for j in (2, 3):
            bz(z_mid, j, z_mid2, False)
            bz(z_mid, j, z_end, True)

    a_forward(z, 0)

    @pl.when(is_end)
    def _():
        got_az(z_mid2)

    a_own(z_mid2)

    @pl.when(is_mid)
    def _():
        got_az(z_end2)
        az(z_end2, z_end, True)

    a_forward(near, 1)

    @pl.when(is_mid)
    def _():
        for j in range(4):
            got_bz(z_end, j)
            bz(z_end, j, z_mid2, False)
        for j in range(4):
            got_bz(z_mid2, j)
            bz(z_mid2, j, z_end, True)

    @pl.when(is_end)
    def _():
        got_az(z_end2)

    a_own(z_end2)
    a_forward(z_mid2, 0)

    @pl.when(is_mid)
    def _():
        for j in range(4):
            got_bz(z_end2, j)
            bz(z_end2, j, z_end, True)

    got_nm = norms.at[m, pl.ds(0, 12)]
    remote(got_nm, got_nm, nm_send.at[0], nm_recv.at[1], plane[0]).wait_recv()
    whole = norms.at[m]
    remote(whole, whole, nm_send.at[1], nm_recv.at[2], partner).start()

    a_forward(z_end2, 1)

    @pl.when(is_end)
    def _():
        for zz in (z_mid, z_mid2, z_end2):
            for j in range(4):
                got_bz(zz, j)

    diagonal = span(4 * tiles(piece_a))
    remote(diagonal, diagonal, send.at[0], recv.at[DIAG], plane[0]).wait_recv()
    theirs = norms.at[1 - m]
    remote(theirs, theirs, nm_send.at[1], nm_recv.at[2], partner).wait_recv()
    sums = mx.at[pl.ds(0, 6)]
    remote(sums, sums, mx_send.at[0], mx_recv.at[0], plane[0]).wait_send()
    tags = norms.at[m, pl.ds(0, 15)]
    remote(tags, tags, nm_send.at[0], nm_recv.at[0], plane[0]).wait_send()
    remote(theirs, theirs, nm_send.at[1], nm_recv.at[2], partner).wait_send()
    remote(early, early, early_send.at[0], early_recv.at[0], plane[0]).wait_send()
    sent(AX_SENT, 4 * tiles(piece_a))
    sent(AY_SENT, 4 * tiles(piece_a))
    sent(FX_SENT, 2 * tiles(for_x[0]) + 2 * tiles(for_x[1]))
    sent(FY_SENT, 2 * tiles(for_y[0]) + 2 * tiles(for_y[1]))
    sent(BX_SENT, tiles(tail_b) + tiles(b_for_x))
    sent(BY_SENT, tiles(tail_b) + tiles(b_for_y))

    @pl.when(is_end)
    def _():
        sent(IN_A, tiles(piece_a))
        sent(IN_B, 4 * tiles(piece_b))

    @pl.when(is_mid)
    def _():
        sent(IN_A, 2 * tiles(piece_a))
        sent(IN_B, 8 * tiles(piece_b))
        sent(OUT_A, 3 * tiles(piece_a))
        sent(OUT_B, 12 * tiles(piece_b))


def write_kernel(length, held, fresh, factor, norms, *rest):
    serve, rates, fresh_out, norm_out, flat, norm_row, sems = rest[:3], rest[3:6], rest[6:9], *rest[9:]
    n = held.shape[0]
    cut = max(1, n // 4)
    start = 0
    for k in range(3):
        cols = pl.ds(start, serve[k].shape[2])
        for b in range(0, n, cut):
            pltpu.make_async_copy(held.at[pl.ds(b, cut), :, cols], serve[k].at[pl.ds(b, cut)], sems.at[0]).start()
        pltpu.make_async_copy(fresh.at[:, cols], fresh_out[k], sems.at[1]).start()
        pltpu.make_async_copy(factor.at[:, cols], rates[k], sems.at[2]).start()
        start += serve[k].shape[2]
    at = 0
    for b in range(n):
        for c in range(norms.shape[0]):
            flat[:, at : at + length] = norms[c, b, :, :length]
            at += length
    norm_row[...] = flat[...].astype(jnp.bfloat16).reshape(at)
    last = pltpu.make_async_copy(norm_row, norm_out, sems.at[3])
    last.start()
    for k, whole in enumerate((held, fresh, factor)):
        pltpu.make_async_copy(whole, whole, sems.at[k]).wait()
    last.wait()


def with_kernel(part_a, split, *args):
    (tq, dq, sq, tk, dk, sk, tv, dv, sv, norm_train, norm_step) = args
    length = norm_train.shape[0]
    padded = -(-length // LANES) * LANES
    n, cores = lax.axis_size("fsdp"), lax.axis_size("model")
    rows = tq.shape[0]
    widths = (tq.shape[1], tk.shape[1], tv.shape[1])
    width = sum(widths)
    vmem = pl.BlockSpec(memory_space=pltpu.VMEM)
    hbm = pl.BlockSpec(memory_space=pltpu.HBM)
    f32, bf16 = jnp.float32, jnp.bfloat16
    room = VMEM_BYTES - n * rows * width * 2 - rows * width * 4 - 192 * 1024
    held, fresh, factor, norms = pl.pallas_call(
        functools.partial(gather_kernel, part_a, split, widths),
        out_shape=(
            pltpu.VMEM((n, rows, width), bf16),
            pltpu.VMEM((rows, width), f32),
            pltpu.VMEM((1, width), f32),
            pltpu.VMEM((cores, n, 1, padded), f32),
        ),
        in_specs=[hbm] * 11,
        out_specs=(vmem,) * 4,
        scratch_shapes=[
            pltpu.VMEM((3, rows, width), f32),
            pltpu.VMEM((2, 1, length), f32),
            pltpu.VMEM((8, width), f32),
            pltpu.VMEM((2, EARLY, width), f32),
            pltpu.VMEM((8, 1, width), f32),
            pltpu.SemaphoreType.DMA((1,)),
            pltpu.SemaphoreType.DMA((rows // CHUNK,)),
            pltpu.SemaphoreType.DMA((2,)),
            pltpu.SemaphoreType.DMA((1,)),
            pltpu.SemaphoreType.DMA((4,)),
            pltpu.SemaphoreType.DMA((2,)),
            pltpu.SemaphoreType.DMA((3,)),
            pltpu.SemaphoreType.DMA((1,)),
            pltpu.SemaphoreType.DMA((2,)),
            pltpu.SemaphoreType.DMA((KINDS,)),
            pltpu.SemaphoreType.DMA((COUNT,)),
        ],
        compiler_params=pltpu.CompilerParams(
            collective_id=0, has_side_effects=True, vmem_limit_bytes=room
        ),
        name="gather",
    )(
        tq, dq, sq, tk, dk, sk, tv, dv, sv,
        norm_train.reshape(1, length), norm_step.reshape(1, length),
    )
    out = pl.pallas_call(
        functools.partial(write_kernel, length),
        out_shape=(
            *[jax.ShapeDtypeStruct((n, rows, w), bf16) for w in widths],
            *[jax.ShapeDtypeStruct((1, w), f32) for w in widths],
            *[jax.ShapeDtypeStruct((rows, w), f32) for w in widths],
            jax.ShapeDtypeStruct((n * cores * length,), bf16),
        ),
        in_specs=[vmem] * 4,
        out_specs=(hbm,) * 10,
        scratch_shapes=[
            pltpu.VMEM((1, n * cores * length), f32),
            pltpu.VMEM((n * cores * length,), bf16),
            pltpu.SemaphoreType.DMA((4,)),
        ],
        compiler_params=pltpu.CompilerParams(vmem_limit_bytes=4 * 1024 * 1024),
        name="write",
    )(held, fresh, factor, norms)
    return (
        *[a.reshape(n * rows, w) for a, w in zip(out[:3], widths)],
        *[a.reshape(w) for a, w in zip(out[3:6], widths)],
        out[9], *out[6:9],
    )


def per_device(
    train_query,
    drift_query,
    spread_query,
    train_key,
    drift_key,
    spread_key,
    train_value,
    drift_value,
    spread_value,
    norm_train,
    norm_step,
):
    n, cores, rows = lax.axis_size("fsdp"), lax.axis_size("model"), train_query.shape[0]
    split = LEAD * LANES
    part_a = (rows - rows // SUB // 4 * SUB, rows - rows // SUB // 5 * SUB)
    lanes_ok = all(a.shape[1] % LANES == 0 for a in (train_query, train_key, train_value))
    if n == 16 and cores == 2 and rows % CHUNK == 0 and part_a[1] + EARLY <= rows and lanes_ok:
        return with_kernel(
            part_a, split,
            train_query, drift_query, spread_query,
            train_key, drift_key, spread_key,
            train_value, drift_value, spread_value,
            norm_train, norm_step,
        )
    fresh_query = train_query - learn_rate * (
        drift_query / (jnp.sqrt(spread_query) + tiny_value) + decay_rate * train_query
    )
    fresh_key = train_key - learn_rate * (
        drift_key / (jnp.sqrt(spread_key) + tiny_value) + decay_rate * train_key
    )
    fresh_value = train_value - learn_rate * (
        drift_value / (jnp.sqrt(spread_value) + tiny_value) + decay_rate * train_value
    )
    factor_query, factor_key, factor_value = lax.pmax(
        (
            jnp.max(jnp.abs(fresh_query), axis=0),
            jnp.max(jnp.abs(fresh_key), axis=0),
            jnp.max(jnp.abs(fresh_value), axis=0),
        ),
        "fsdp",
    )
    narrow_query, narrow_key, narrow_value = (
        (fresh_query / factor_query).astype(jnp.bfloat16),
        (fresh_key / factor_key).astype(jnp.bfloat16),
        (fresh_value / factor_value).astype(jnp.bfloat16),
    )
    serve_query, serve_key, serve_value = (
        lax.all_gather(narrow_query, "fsdp", axis=0, tiled=True),
        lax.all_gather(narrow_key, "fsdp", axis=0, tiled=True),
        lax.all_gather(narrow_value, "fsdp", axis=0, tiled=True),
    )
    serve_norm = lax.all_gather(
        (norm_train + norm_step).astype(jnp.bfloat16), ("fsdp", "model"), axis=0, tiled=True
    )
    return (
        serve_query,
        serve_key,
        serve_value,
        factor_query,
        factor_key,
        factor_value,
        serve_norm,
        fresh_query,
        fresh_key,
        fresh_value,
    )


def solution(mesh):
    in_specs = (
        P("fsdp", "model"),
        P("fsdp", "model"),
        P("fsdp", "model"),
        P("fsdp", "model"),
        P("fsdp", "model"),
        P("fsdp", "model"),
        P("fsdp", "model"),
        P("fsdp", "model"),
        P("fsdp", "model"),
        P(("fsdp", "model")),
        P(("fsdp", "model")),
    )
    out_specs = (
        P(None, "model"),
        P(None, "model"),
        P(None, "model"),
        P("model"),
        P("model"),
        P("model"),
        P(),
        P("fsdp", "model"),
        P("fsdp", "model"),
        P("fsdp", "model"),
    )
    return jax.shard_map(
        per_device, mesh=mesh, in_specs=in_specs, out_specs=out_specs, check_vma=False
    )
```

time: 127 us -> 124 us (0.976)
  Pallas kernels: 126 us -> 124 us
    pallas_call x1, Pallas kernels: 120 us -> 117 us  [with_kernel(): pl.pallas_call(functools.partial(gather_kernel, part_a, split, widths), o...]
where the time goes in v2:
time: 124 us
  Pallas kernels  124 us (100%)
    pallas_call x1, Pallas kernels, with_kernel(): pl.pallas_call(functools.partial(gather_kernel, part_a, split, widths), o...  117 us
    pallas_call x1, Pallas kernels, with_kernel(): pl.pallas_call(functools.partial(write_kernel, length), out_shape=(*[jax....  6.15 us

profile of v2, /device:TPU:0, one launch (start us, length us, event | category | flops | bytes accessed | tf_op | source)
XLA Modules:
  0.0 124.2 jit_solution(189041661729167745)
XLA Ops:
  0.6 117.4 %gather.1 = (bf16[16,160,3072]{2,1,0:T(8,128)(2,1)S(1)}, f32[160,3072]{1,0:T(8,128)S(1)}, f32[1,3072]{1,0:T(1,128)S(1)}, f32[2,16,1,128]{3,2,1,0:T(1,128)S(1)}) custom-call(f32[160,2048]{1,0:T(8,128)} %tq.1, f32[160,2048]{1,0:T(8,128)} %dq.1, f32[160,2048]{1,0:T(8,128)} %sq.1, f32[160,512]{1,0:T(8,128)} %tk.1, f32[160,512]{1,0:T(8,128)} %dk.1, ...), custom_call_target="tpu_custom_call" | custom-call | tf_op jit(solution)/shard_map/gather/pallas_call | solution.py:430
  118.0 6.1 %write.1 = (bf16[16,160,2048]{2,1,0:T(8,128)(2,1)}, bf16[16,160,512]{2,1,0:T(8,128)(2,1)}, bf16[16,160,512]{2,1,0:T(8,128)(2,1)}, f32[1,2048]{1,0:T(1,128)}, f32...) custom-call(bf16[16,160,3072]{2,1,0:T(8,128)(2,1)S(1)} %get-tuple-el, ...), custom_call_target="tpu_custom_call" | custom-call | tf_op jit(solution)/shard_map/write/pallas_call | solution.py:466
